TPU v7x, 32 devices: a whole 2x2x4 slice. The times are simulated.
32 devices in a mesh: dp: 4 (over x, core), tensor: 8 (over z, y).
Axes of the slice: x: 2, y: 2, z: 4, core: 2. Of those that a mesh axis runs over, the one named last changes fastest.
Arguments:
- hidden: bfloat16 [8, 64, 4608], P('dp', 'tensor'), may hold values from -6 to 6
- gain: float32 [4608], replicated, may hold values from 0.5 to 1.5
- labels: int32 [8, 64], P('dp', 'tensor'), may hold values from 0 to 255999
- lengths: int32 [8], replicated, may hold values from 1 to 64
- embed: bfloat16 [256000, 4608], P(('dp', 'tensor')), may hold values from -0.375 to 0.375
Outputs:
- token_logprob: float32 [8, 64], P('dp', 'tensor')
- mean_nll: float32 [], replicated
- z_loss: float32 [], replicated
All inputs are finite; a program needn't handle non-finite values.
Results may differ from a plain program's by a relative error of at most 0.00058.
Values may be sent and summed in bfloat16 or wider, within the bound.
A program may use at most 128 MiB of HBM per device.

v0:
```python
import jax
import jax.numpy as jnp
from jax import lax
from jax.sharding import PartitionSpec as P

CAP = 30


def normalize(rows, gain):
    values = rows.astype(jnp.float32)
    meansq = jnp.mean(values * values, axis=-1, keepdims=True)
    return (values * lax.rsqrt(meansq + 1e-06) * gain).astype(jnp.bfloat16)


def per_device(hidden, gain, labels, lengths, embed):
    n_tensor = lax.axis_size("tensor")
    n_all = lax.axis_size("dp") * n_tensor
    seqs, stretch, width = hidden.shape
    vocab_dev = embed.shape[0]
    rows_local = seqs * stretch
    total_rows = rows_local * n_all
    flat = hidden.reshape(rows_local, width)
    row_ids = jnp.arange(total_rows)
    owner = row_ids // rows_local
    within = row_ids % rows_local
    batch_ids = owner // n_tensor * seqs + within // stretch
    positions = owner % n_tensor * stretch + within % stretch
    live_all = (positions < jnp.take(lengths, batch_ids)).astype(jnp.float32)
    all_labels = lax.all_gather(labels.reshape(rows_local), ("dp", "tensor"), axis=0, tiled=True)
    outgoing = normalize(flat, gain)
    rows = lax.all_gather(outgoing, ("dp", "tensor"), axis=0, tiled=True)
    values = lax.dot_general(
        rows, embed, (((1,), (1,)), ((), ())), preferred_element_type=jnp.float32
    )
    capped = CAP * jnp.tanh(values / CAP)
    sumexp = jnp.sum(jnp.exp(capped), axis=1)
    first = lax.axis_index(("dp", "tensor")) * vocab_dev
    local = all_labels - first
    inside = (local >= 0) & (local < vocab_dev)
    chosen = jnp.take_along_axis(capped, jnp.clip(local, 0, vocab_dev - 1)[:, None], axis=1)[:, 0]
    picked = jnp.where(inside, chosen, jnp.float32(0.0))
    own_start = lax.axis_index(("dp", "tensor")) * rows_local
    sum_total, pick_total = lax.psum((sumexp, picked), ("dp", "tensor"))
    own_sum = lax.dynamic_slice_in_dim(sum_total, own_start, rows_local)
    own_pick = lax.dynamic_slice_in_dim(pick_total, own_start, rows_local)
    own_live = lax.dynamic_slice_in_dim(live_all, own_start, rows_local)
    lse = jnp.log(own_sum)
    token = own_live * (own_pick - lse)
    nll_sum, count, square_sum = lax.psum(
        (-jnp.sum(token), jnp.sum(own_live), jnp.sum(own_live * lse * lse)), ("dp", "tensor")
    )
    mean_nll = nll_sum / count
    z_loss = 0.01 * square_sum / count
    return (token.reshape(seqs, stretch), mean_nll, z_loss)


def solution(mesh):
    return jax.shard_map(
        per_device,
        mesh=mesh,
        in_specs=(P("dp", "tensor", None), P(), P("dp", "tensor"), P(), P(("dp", "tensor"), None)),
        out_specs=(P("dp", "tensor"), P(), P()),
        check_vma=False,
    )
```

profile of v0, /device:TPU:0, one launch (start us, length us, event | category | flops | bytes accessed | tf_op | source)
XLA Modules:
  0.0 240.6 jit_solution(1555822703838976775)
XLA Ops:
  7.2 0.0 all-gather.2.cloned.1.call-start
  7.2 1.0 fusion.3
  8.3 0.1 rsqrt.12
  8.3 1.7 fusion.2
  10.0 0.0 all-gather.2.cloned.1.call-update
  10.0 0.8 reshape.263
  10.8 0.2 dynamic-update-slice
  11.0 42.2 %all-reduce = s32[512]{0:T(512)S(1)} all-reduce(s32[512]{0:T(512)S(1)} %dynamic-update-slice), channel_id=1, replica_groups=mesh['dp'=4,'tensor'=8] {'dp','tensor'}, use_global_device_ids=true, to_apply=%add | all-reduce | flops 512 | bytes 4096
  53.2 1.6 fusion.29
  54.8 4.5 %compare_select_fusion.1 = s32[512,1]{0,1:T(1,128)S(1)} fusion(s32[]{:T(128)} %bitcast.1, s32[]{:T(128)} %bitcast.2, s32[]{:T(128)} %bitcast.3, s32[]{:T(128)} %bitcast.4, s32[]{:T(128)} %bitcast.5, s32[]{:T(128)} %bitcast.7, s32[]{:T(128)} %bitcast.6), kind=kLoop, calls=%fused_computation.11 | loop fusion | flops 30208 | bytes 2076 | tf_op jit(solution)/shard_map/jit(_take)/gather | solution.py:28
  59.4 0.7 fusion.26
  60.1 17.2 %all-gather.2.cloned.1.call-done = bf16[512,4608]{1,0:T(8,128)(2,1)} async-done(((bf16[16,4608]{1,0:T(8,128)(2,1)}), bf16[512,4608]{1,0:T(8,128)(2,1)}) %all-gather.2.cloned.1.call-update) | async-done | bytes 4718608 | tf_op jit(solution)/shard_map/all_gather | solution.py:31
  77.3 48.5 %exponential_reduce_fusion = (f32[512]{0:T(512)S(1)}, f32[512,8000]{0,1:T(8,128)}) fusion(bf16[512,4608]{1,0:T(8,128)(2,1)} %all-gather.2.cloned.1.call-done, bf16[8000,4608]{1,0:T(8,128)(2,1)} %param.9), kind=kOutput, calls=%fused_computation.1 | convolution fusion | flops 37761024000 | bytes 94832640 | tf_op jit(solution)/shard_map/dot_general | solution.py:32
  125.8 22.4 %gather_fusion = f32[512]{0:T(512)S(1)} fusion(f32[512,8000]{0,1:T(8,128)} %get-tuple-element.23, s32[512]{0:T(512)S(1)} %bitcast.23), kind=kCustom, calls=%fused_computation | custom fusion | bytes 8192 | tf_op jit(solution)/shard_map/jit(take_along_axis)/gather | solution.py:40
  148.2 37.6 %all-reduce.2 = (f32[512]{0:T(512)S(1)}, f32[512]{0:T(512)S(1)}) all-reduce(f32[512]{0:T(512)S(1)} %select_select_fusion.1, f32[512]{0:T(512)S(1)} %get-tuple-element.22), channel_id=1, replica_groups=mesh['dp'=4,'tensor'=8] {'dp','tensor'}, use_global_device_ids=true, to_apply=%region_1.2 | all-reduce | flops 1024 | bytes 8192 | tf_op jit(solution)/shard_map/psum | solution.py:43
  185.8 0.8 fusion.27
  186.6 0.6 reshape.216
  187.9 41.0 %all-reduce.1 = (f32[]{:T(128)}, f32[]{:T(128)}, f32[]{:T(128)}) all-reduce(f32[]{:T(128)S(6)} %neg.3, f32[]{:T(128)} %get-tuple-element.4, f32[]{:T(128)} %get-tuple-element.3), channel_id=1, replica_groups=mesh['dp'=4,'tensor'=8] {'dp','tensor'}, use_global_device_ids=true, to_apply=%region_5.6 | all-reduce | flops 3 | bytes 24 | tf_op jit(solution)/shard_map/psum | solution.py:49
  (8 shorter events, 0.1 us)
Async XLA Ops:
  7.2 70.1 %all-gather.2.cloned.1.call-start = ((), (), s32[]{:S(2)}) async-start(), calls=%async_computation | async-start | bytes 4866048 | tf_op jit(solution)/shard_map/all_gather | solution.py:31
Sparse Core Ops, SparseCore 0:
  10.9 66.3 all-gather.1
where the time goes:
time: 241 us
  blocking collectives  121 us (50%)
  matrix products  48.5 us (20%)
  local copies, waits for them, and re-layouts  25.7 us (11%)
  between operations  19.6 us (8%)
  waiting for transfers between devices  17.2 us (7%)
  other arithmetic  8.75 us (4%)
    dot_general x1, matrix products, per_device(): lax.dot_general(rows, embed, (((1,), (1,)), ((), ())), preferred_element_...  48.5 us
    unnamed x1, blocking collectives  42.2 us
    psum x1, blocking collectives, per_device(): lax.psum((-jnp.sum(token), jnp.sum(own_live), jnp.sum(own_live * lse * ls...  41 us
    psum x1, blocking collectives, per_device(): sum_total, pick_total = lax.psum((sumexp, picked), ('dp', 'tensor'))  37.6 us
    gather x1, local copies, waits for them, and re-layouts, per_device(): jnp.take_along_axis(capped, jnp.clip(local, 0, vocab_dev - 1)[:, None], a...  22.4 us
    all_gather x1, waiting for transfers between devices, per_device(): rows = lax.all_gather(outgoing, ('dp', 'tensor'), axis=0, tiled=True)  17.2 us
  transfers between devices with their start and end apart: 1, of which 1 were waited for; matrix products, arithmetic and copies ran while one was open for 3% of the time, Pallas kernels for 0%

commit v1 on v0

--- a/solution.py
+++ b/solution.py
@@ -40,7 +40,7 @@
     chosen = jnp.take_along_axis(capped, jnp.clip(local, 0, vocab_dev - 1)[:, None], axis=1)[:, 0]
     picked = jnp.where(inside, chosen, jnp.float32(0.0))
     own_start = lax.axis_index(("dp", "tensor")) * rows_local
-    sum_total, pick_total = lax.psum((sumexp, picked), ("dp", "tensor"))
+    sum_total, pick_total = lax.psum(lax.psum((sumexp, picked), "tensor"), "dp")
     own_sum = lax.dynamic_slice_in_dim(sum_total, own_start, rows_local)
     own_pick = lax.dynamic_slice_in_dim(pick_total, own_start, rows_local)
     own_live = lax.dynamic_slice_in_dim(live_all, own_start, rows_local)

time: 241 us -> 224 us (0.929)
  blocking collectives: 121 us -> 103 us
    psum x1 -> x2, blocking collectives: 37.6 us -> 23.7 us  [per_device(): sum_total, pick_total = lax.psum(lax.psum((sumexp, picked), 'tensor'), 'dp')]
    psum x1, blocking collectives: 41 us -> 37.1 us  [per_device(): lax.psum((-jnp.sum(token), jnp.sum(own_live), jnp.sum(own_live * lse * ls...]
  transfers between devices with their start and end apart: 1 -> 1, of which waited for: 1 -> 1; matrix products, arithmetic and copies ran while one was open for 3% -> 4% of each run, Pallas kernels for 0% -> 0%
where the time goes in v1:
time: 224 us; the launch traced here: 223 us
  blocking collectives  103 us (46%)
  matrix products  48.5 us (22%)
  local copies, waits for them, and re-layouts  25.7 us (11%)
  between operations  19.6 us (9%)
  waiting for transfers between devices  17.2 us (8%)
  other arithmetic  8.75 us (4%)
    dot_general x1, matrix products, per_device(): lax.dot_general(rows, embed, (((1,), (1,)), ((), ())), preferred_element_...  48.5 us
    unnamed x1, blocking collectives  42.2 us
    psum x1, blocking collectives, per_device(): lax.psum((-jnp.sum(token), jnp.sum(own_live), jnp.sum(own_live * lse * ls...  37.1 us
    psum x2, blocking collectives, per_device(): sum_total, pick_total = lax.psum(lax.psum((sumexp, picked), 'tensor'), 'dp')  23.7 us
    gather x1, local copies, waits for them, and re-layouts, per_device(): jnp.take_along_axis(capped, jnp.clip(local, 0, vocab_dev - 1)[:, None], a...  22.4 us
    all_gather x1, waiting for transfers between devices, per_device(): rows = lax.all_gather(outgoing, ('dp', 'tensor'), axis=0, tiled=True)  17.2 us
    gather x2, other arithmetic, per_device(): live_all = (positions < jnp.take(lengths, batch_ids)).astype(jnp.float32)  4.56 us
  transfers between devices with their start and end apart: 1, of which 1 were waited for; matrix products, arithmetic and copies ran while one was open for 4% of the time, Pallas kernels for 0%

profile of v1, /device:TPU:0, one launch (start us, length us, event | category | flops | bytes accessed | tf_op | source)
XLA Modules:
  0.0 222.8 jit_solution(1924517840298856229)
XLA Ops:
  7.2 0.0 all-gather.2.cloned.1.call-start
  7.2 1.0 fusion.3
  8.3 0.1 rsqrt.12
  8.3 1.7 fusion.2
  10.0 0.0 all-gather.2.cloned.1.call-update
  10.0 0.8 reshape.263
  10.8 0.2 dynamic-update-slice
  11.0 42.2 %all-reduce = s32[512]{0:T(512)S(1)} all-reduce(s32[512]{0:T(512)S(1)} %dynamic-update-slice), channel_id=1, replica_groups=mesh['dp'=4,'tensor'=8] {'dp','tensor'}, use_global_device_ids=true, to_apply=%add | all-reduce | flops 512 | bytes 4096
  53.2 1.6 fusion.29
  54.8 4.5 %compare_select_fusion.1 = s32[512,1]{0,1:T(1,128)S(1)} fusion(s32[]{:T(128)} %bitcast.1, s32[]{:T(128)} %bitcast.2, s32[]{:T(128)} %bitcast.3, s32[]{:T(128)} %bitcast.4, s32[]{:T(128)} %bitcast.5, s32[]{:T(128)} %bitcast.7, s32[]{:T(128)} %bitcast.6), kind=kLoop, calls=%fused_computation.11 | loop fusion | flops 30208 | bytes 2076 | tf_op jit(solution)/shard_map/jit(_take)/gather | solution.py:28
  59.4 0.7 fusion.26
  60.1 17.2 %all-gather.2.cloned.1.call-done = bf16[512,4608]{1,0:T(8,128)(2,1)} async-done(((bf16[16,4608]{1,0:T(8,128)(2,1)}), bf16[512,4608]{1,0:T(8,128)(2,1)}) %all-gather.2.cloned.1.call-update) | async-done | bytes 4718608 | tf_op jit(solution)/shard_map/all_gather | solution.py:31
  77.3 48.5 %exponential_reduce_fusion = (f32[512]{0:T(512)S(1)}, f32[512,8000]{0,1:T(8,128)}) fusion(bf16[512,4608]{1,0:T(8,128)(2,1)} %all-gather.2.cloned.1.call-done, bf16[8000,4608]{1,0:T(8,128)(2,1)} %param.9), kind=kOutput, calls=%fused_computation.1 | convolution fusion | flops 37761024000 | bytes 94832640 | tf_op jit(solution)/shard_map/dot_general | solution.py:32
  125.8 22.4 %gather_fusion = f32[512]{0:T(512)S(1)} fusion(f32[512,8000]{0,1:T(8,128)} %get-tuple-element.25, s32[512]{0:T(512)S(1)} %bitcast.23), kind=kCustom, calls=%fused_computation | custom fusion | bytes 8192 | tf_op jit(solution)/shard_map/jit(take_along_axis)/gather | solution.py:40
  148.2 17.9 %all-reduce.2 = (f32[512]{0:T(512)S(1)}, f32[512]{0:T(512)S(1)}) all-reduce(f32[512]{0:T(512)S(1)} %select_select_fusion.1, f32[512]{0:T(512)S(1)} %get-tuple-element.24), channel_id=1, replica_groups=mesh['dp'=4,'tensor'=8] {'tensor'}, use_global_device_ids=true, to_apply=%region_1.2 | all-reduce | flops 1024 | bytes 8192 | tf_op jit(solution)/shard_map/psum | solution.py:43
  166.1 5.7 %all-reduce.3 = (f32[512]{0:T(512)S(1)}, f32[512]{0:T(512)S(1)}) all-reduce(f32[512]{0:T(512)S(1)} %get-tuple-element.8, f32[512]{0:T(512)S(1)} %get-tuple-element.9), channel_id=1, replica_groups=mesh['dp'=4,'tensor'=8] {'dp'}, use_global_device_ids=true, to_apply=%region_2.3 | all-reduce | flops 1024 | bytes 8192 | tf_op jit(solution)/shard_map/psum | solution.py:43
  171.9 0.8 fusion.27
  172.6 0.6 reshape.216
  174.0 37.1 %all-reduce.1 = (f32[]{:T(128)}, f32[]{:T(128)}, f32[]{:T(128)}) all-reduce(f32[]{:T(128)S(6)} %neg.3, f32[]{:T(128)} %get-tuple-element.4, f32[]{:T(128)} %get-tuple-element.3), channel_id=1, replica_groups=mesh['dp'=4,'tensor'=8] {'dp','tensor'}, use_global_device_ids=true, to_apply=%region_7.8 | all-reduce | flops 3 | bytes 24 | tf_op jit(solution)/shard_map/psum | solution.py:49
  (8 shorter events, 0.1 us)
Async XLA Ops:
  7.2 70.1 %all-gather.2.cloned.1.call-start = ((), (), s32[]{:S(2)}) async-start(), calls=%async_computation | async-start | bytes 4866048 | tf_op jit(solution)/shard_map/all_gather | solution.py:31
Sparse Core Ops, SparseCore 0:
  10.9 66.3 all-gather.1
